TPU v7x, 32 devices: a whole 2x2x4 slice. The times are simulated.
32 devices in a mesh: tok: 4 (over y, x), hid: 2 (over core), voc: 4 (over z).
Axes of the slice: x: 2, y: 2, z: 4, core: 2. Of those that a mesh axis runs over, the one named last changes fastest.
Arguments:
- student_hidden: bfloat16 [512, 8192], P('tok', ('hid', 'voc')), may hold values from -8 to 8
- teacher_hidden: bfloat16 [512, 16384], P('tok', ('hid', 'voc')), may hold values from -8 to 8
- student_head: bfloat16 [8192, 2048], P('hid', 'voc'), may hold values from -2 to 2
- teacher_head: bfloat16 [16384, 2048], P('hid', 'voc'), may hold values from -2 to 2
- loss_weight: float32 [512], P('tok'), may hold values from 128 to 1024
Outputs:
- grad_hidden: bfloat16 [512, 8192], P('tok', ('hid', 'voc'))
- mean_loss: float32 [], replicated
All inputs are finite; a program needn't handle non-finite values.
Results may differ from a plain program's by a relative error of at most 0.001.
The roundings to bfloat16 on the way count: a program that leaves them out, or rounds other values in their place, can miss the bound.
Values may be sent and summed in bfloat16 or wider, within the bound.
A program may use at most 64 MiB of HBM per device.

v0:
```python
import functools

import jax
import jax.numpy as jnp
from jax import lax
from jax.experimental import pallas as pl
from jax.experimental.pallas import tpu as pltpu
from jax.sharding import PartitionSpec as P

MESH = pl.DeviceIdType.MESH
F32 = jnp.float32
BF16 = jnp.bfloat16


def fused(n, nt, x_hbm, y_hbm, w_hbm, sw_hbm, tw_hbm, out, loss_out,
          x_ref, y_ref, w_ref, wf, tw, tg, sp, spx, ssum, srr, tacc, tpx, stat, gap, wcol, lossb, acc,
          lc, wz_s, wz_r, wt_s, wt_r, th_s, th_r, px_s, px_r, rs_s, rs_r,
          st_s, st_r, gz_s, gz_r, gx_s, gx_r, ls_s, ls_r):
    z = lax.axis_index("voc")
    t = lax.axis_index("tok")
    h = lax.axis_index("hid")
    rows, ks = x_ref.shape
    kt = y_ref.shape[1]
    half = rows // 2
    quarter = ks // nt
    partner = {"hid": 1 - h}
    mine = pl.ds(pl.multiple_of(h * half, half), half)
    theirs = pl.ds(pl.multiple_of((1 - h) * half, half), half)
    me = t * 2 + h

    def rc(src, dst, ss, rs, dev):
        return pltpu.make_async_remote_copy(
            src_ref=src, dst_ref=dst, send_sem=ss, recv_sem=rs,
            device_id=dev, device_id_type=MESH)

    def zdev(k):
        return lax.rem(z + k, n)

    plane = []
    for q in range(nt):
        for c in range(2):
            if q or c:
                plane.append((lax.rem(t + q, nt), lax.rem(h + c, 2)))

    own_w = pltpu.make_async_copy(sw_hbm.at[pl.ds(pl.multiple_of(z * ks, ks), ks)], wf.at[z], lc.at[n])
    own_w.start()
    ins = [pltpu.make_async_copy(a, b, lc.at[n + 1 + i])
           for i, (a, b) in enumerate(((x_hbm, x_ref), (y_hbm, y_ref), (w_hbm, w_ref)))]
    for c in ins:
        c.start()

    def tw_copy(i):
        return pltpu.make_async_copy(tw_hbm.at[pl.ds(pl.multiple_of(i * kt, kt), kt)], tw.at[i], lc.at[i])

    barrier = pltpu.get_barrier_semaphore()
    for k in range(1, n):
        pl.semaphore_signal(barrier, inc=1, device_id={"voc": zdev(k)}, device_id_type=MESH)
    for (a, b) in plane:
        pl.semaphore_signal(barrier, inc=1, device_id={"tok": a, "hid": b}, device_id_type=MESH)
    pl.semaphore_wait(barrier, n - 1 + len(plane))

    def part(i):
        return pl.ds(pl.multiple_of(i * quarter, quarter), quarter)

    def wz(j):
        return rc(sw_hbm.at[pl.ds(pl.multiple_of(j * ks + t * quarter, quarter), quarter)],
                  wf.at[z, part(t)], wz_s.at[j], wz_r.at[z], {"voc": j})

    def wz_in(j):
        return rc(wf.at[j, part(t)], wf.at[j, part(t)], wz_s.at[j], wz_r.at[j], {"voc": j})

    def wt(j, dst_t):
        return rc(wf.at[j, part(t)], wf.at[j, part(t)], wt_s.at[j, dst_t], wt_r.at[j, t], {"tok": dst_t})

    def wt_in(j, src_t):
        return rc(wf.at[j, part(src_t)], wf.at[j, part(src_t)], wt_s.at[j, src_t], wt_r.at[j, src_t], {"tok": src_t})

    def sides(d):
        return ((z - d, z - d >= 0), (z + d, z + d < n))

    for d in range(n - 1, 0, -1):
        for j, ok in sides(d):
            @pl.when(ok)
            def _(j=j):
                wz(j).start()

    def piece(r):
        return pl.ds(r * half, half)

    def own_y(r, side):
        return rc(y_hbm.at[piece(r)], tg.at[z, piece(r)], th_s.at[side, z, r], th_r.at[z, r],
                  {"voc": z + (1 if side else -1)})

    def relay_y(i, r, side):
        return rc(tg.at[i, piece(r)], tg.at[i, piece(r)], th_s.at[side, i, r], th_r.at[i, r],
                  {"voc": z + (1 if side else -1)})

    room = (z - 1 >= 0, z + 1 < n)
    for r in range(2):
        for side in range(2):
            @pl.when(room[side])
            def _(r=r, side=side):
                own_y(r, side).start()

    for k in range(n):
        tw_copy(zdev(k)).start()

    for c in ins:
        c.wait()
    wcol[...] = jnp.transpose(jnp.broadcast_to(w_ref[...], (rows, rows)))

    for d in range(n - 1, 0, -1):
        for j, ok in sides(d):
            @pl.when(ok)
            def _(j=j):
                wz_in(j).wait_recv()
                for q in range(1, nt):
                    wt(j, lax.rem(t + q, nt)).start()

    def teacher_dot(src, i, first):
        tw_copy(i).wait()
        step = kt // 2

        @pl.loop(0, 2)
        def _(s):
            cols = pl.ds(pl.multiple_of(s * step, step), step)
            term = jnp.dot(src[:, cols], tw[i, cols, :], preferred_element_type=F32)
            if first:
                @pl.when(s == 0)
                def _():
                    tacc[...] = term

                @pl.when(s > 0)
                def _():
                    tacc[...] += term
            else:
                tacc[...] += term

    teacher_dot(y_ref, z, True)

    def take_y(d, dot):
        for r in range(2):
            for side, (i, ok) in enumerate(sides(d)):
                @pl.when(ok)
                def _(i=i, side=side, r=r):
                    relay_y(i, r, side).wait_recv()
                    if d < n - 1:
                        on = 1 - side

                        @pl.when(room[on])
                        def _():
                            relay_y(i, r, on).start()
        if dot:
            dot_y(d)

    def dot_y(d):
        for i, ok in sides(d):
            @pl.when(ok)
            def _(i=i):
                teacher_dot(tg.at[i], i, False)

    def student(j, own):
        if own:
            own_w.wait()
        else:
            for q in range(1, nt):
                wt_in(j, lax.rem(t + q, nt)).wait_recv()
        sp[j] = jnp.dot(x_ref[...], wf[j], preferred_element_type=F32)
        swap = rc(sp.at[j, theirs], spx.at[j], px_s.at[j], px_r.at[j], partner)
        swap.start()
        swap.wait_recv()
        ssum[j] = sp[j, mine, :] + spx[j]

    def rs(side, j):
        return rc(ssum.at[j], srr.at[side, j], rs_s.at[j], rs_r.at[side, j],
                  {"voc": z + (1 if side else -1)})

    def student_step(d):
        for side, (j, ok) in enumerate(sides(d)):
            @pl.when(ok)
            def _(j=j, side=side):
                student(j, False)

                @pl.when(room[1 - side])
                def _():
                    rs(side, j).wait_recv()
                    ssum[j] += srr[side, j]
                rs(side, j).start()

    take_y(1, False)
    student_step(n - 1)
    dot_y(1)
    for d in range(n - 2, 0, -1):
        if d == 1:
            for e in range(2, n - 1):
                take_y(e, True)
        student_step(d)
    student(z, True)
    for side in range(2):
        @pl.when(room[1 - side])
        def _(side=side):
            rs(side, z).wait_recv()
            ssum[z] += srr[side, z]
    sl = ssum[z]
    ms = jnp.max(sl, axis=1, keepdims=True)
    ss = jnp.sum(jnp.exp(sl - ms), axis=1, keepdims=True)
    take_y(n - 1, True)

    tx = rc(tacc.at[theirs], tpx, px_s.at[n], px_r.at[n], partner)
    tx.start()
    tx.wait_recv()
    tl = tacc[mine, :] + tpx[...]
    tpx[...] = tl
    mt = jnp.max(tl, axis=1, keepdims=True)
    et = jnp.exp(tl - mt)
    st = jnp.sum(et, axis=1, keepdims=True)
    cr = jnp.sum(et * (tl - sl), axis=1, keepdims=True)
    lane = lax.broadcasted_iota(jnp.int32, (half, 128), 1)
    cols = jnp.where(lane == 0, ms, jnp.where(lane == 1, mt, jnp.where(
        lane == 2, ss, jnp.where(lane == 3, st, cr))))
    stat[z] = jnp.transpose(jnp.concatenate([cols] * (128 // half), axis=0))[:8]

    def stx(j, src):
        return rc(stat.at[src], stat.at[src], st_s.at[j], st_r.at[src], {"voc": j})

    for k in range(1, n):
        stx(zdev(k), z).start()
    for k in range(1, n):
        stx(zdev(k), zdev(k)).wait_recv()
    parts = [stat[j] for j in range(n)]
    top = parts[0]
    for p in parts[1:]:
        top = jnp.maximum(top, p)
    big_s, big_t = top[0:1], top[1:2]
    tot_s = jnp.zeros_like(big_s)
    tot_t = jnp.zeros_like(big_s)
    cross = jnp.zeros_like(big_s)
    for p in parts:
        es = jnp.exp(p[0:1] - big_s)
        ets = jnp.exp(p[1:2] - big_t)
        tot_s = tot_s + p[2:3] * es
        tot_t = tot_t + p[3:4] * ets
        cross = cross + p[4:5] * ets
    lse_s = big_s + jnp.log(tot_s)
    lse_t = big_t + jnp.log(tot_t)
    scale = wcol[mine, :][:, 0:1]
    sub = lax.broadcasted_iota(jnp.int32, (128, 128), 0)
    back = jnp.transpose(jnp.where(sub == 0, lse_s, lse_t))[:half]
    col_s, col_t = back[:, 0:1], back[:, 1:2]
    gap[z, mine, :] = (scale * (jnp.exp(ssum[z] - col_s) - jnp.exp(tpx[...] - col_t))).astype(BF16)

    def gz(j, src):
        return rc(gap.at[src, mine], gap.at[src, mine], gz_s.at[j], gz_r.at[src], {"voc": j})

    def gx(src, side):
        return rc(gap.at[src, side], gap.at[src, side], gx_s.at[src], gx_r.at[src], partner)

    for d in range(1, n):
        for j, ok in sides(d):
            @pl.when(ok)
            def _(j=j):
                gz(j, z).start()
    gx(z, mine).start()

    div = cross / tot_t - lse_t + lse_s
    first = lax.broadcasted_iota(jnp.int32, div.shape, 1) < half
    lossb[me] = jnp.broadcast_to(jnp.sum(jnp.where(first, div, 0.0), axis=1, keepdims=True), (8, 128))

    def ls(a, b, src):
        return rc(lossb.at[src], lossb.at[src], ls_s.at[a * 2 + b], ls_r.at[src], {"tok": a, "hid": b})

    for (a, b) in plane:
        ls(a, b, me).start()

    def grad_dot(j, first):
        term = lax.dot_general(gap[j], wf[j], (((1,), (1,)), ((), ())), preferred_element_type=F32)
        if first:
            acc[...] = term
        else:
            acc[...] += term

    gx(z, theirs).wait_recv()
    grad_dot(z, True)
    for d in range(1, n):
        for j, ok in sides(d):
            @pl.when(ok)
            def _(j=j):
                gz(j, j).wait_recv()
                gx(j, mine).start()
    for k in range(1, n):
        j = zdev(k)
        gx(j, theirs).wait_recv()
        grad_dot(j, False)
    out[...] = acc[...].astype(BF16)

    for (a, b) in plane:
        ls(a, b, a * 2 + b).wait_recv()
    total = lossb[0]
    for p in range(1, nt * 2):
        total = total + lossb[p]
    loss_out[0, 0] = total[0, 0] / (rows * nt)

    for k in range(1, n):
        j = zdev(k)
        wz(j).wait_send()
        for q in range(1, nt):
            wt(j, lax.rem(t + q, nt)).wait_send()
        rc(ssum.at[j], srr.at[0, j], rs_s.at[j], rs_r.at[0, j], {"voc": j}).wait_send()
        stx(j, z).wait_send()
        gz(j, z).wait_send()
    for r in range(2):
        for side in range(2):
            @pl.when(room[side])
            def _(r=r, side=side):
                own_y(r, side).wait_send()
    for d in range(1, n - 1):
        for r in range(2):
            for side, (i, ok) in enumerate(sides(d)):
                on = 1 - side

                @pl.when(jnp.logical_and(ok, room[on]))
                def _(i=i, r=r, on=on):
                    relay_y(i, r, on).wait_send()
    for k in range(n):
        j = zdev(k)
        rc(sp.at[j, theirs], spx.at[j], px_s.at[j], px_r.at[j], partner).wait_send()
        gx(j, mine).wait_send()
    tx.wait_send()
    for (a, b) in plane:
        ls(a, b, me).wait_send()


def fused_shards(n, nt, student_hidden, teacher_hidden, student_head, teacher_head, loss_weight):
    rows, ks = student_hidden.shape
    kt = teacher_hidden.shape[1]
    v = student_head.shape[1]
    half = rows // 2
    dma = lambda *s: pltpu.SemaphoreType.DMA(s)
    vmem = lambda s, d: pltpu.VMEM(s, d)
    whole = pl.BlockSpec(memory_space=pltpu.VMEM)
    anywhere = pl.BlockSpec(memory_space=pl.ANY)
    grad, loss = pl.pallas_call(
        functools.partial(fused, n, nt),
        out_shape=(jax.ShapeDtypeStruct((rows, ks), BF16), jax.ShapeDtypeStruct((1, 1), F32)),
        in_specs=[anywhere] * 5,
        out_specs=(whole, pl.BlockSpec(memory_space=pltpu.SMEM)),
        scratch_shapes=[
            vmem((rows, ks), BF16),
            vmem((rows, kt), BF16),
            vmem((1, rows), F32),
            vmem((n, ks, v), BF16),
            vmem((n, kt, v), BF16),
            vmem((n, rows, kt), BF16),
            vmem((n, rows, v), F32),
            vmem((n, half, v), F32),
            vmem((n, half, v), F32),
            vmem((2, n, half, v), F32),
            vmem((rows, v), F32),
            vmem((half, v), F32),
            vmem((n, 8, 128), F32),
            vmem((n, rows, v), BF16),
            vmem((rows, rows), F32),
            vmem((nt * 2, 8, 128), F32),
            vmem((rows, ks), F32),
            dma(n + 4),
            dma(n), dma(n), dma(n, nt), dma(n, nt),
            dma(2, n, 2), dma(n, 2),
            dma(n + 1), dma(n + 1), dma(n), dma(2, n),
            dma(n), dma(n), dma(n), dma(n), dma(n), dma(n),
            dma(nt * 2), dma(nt * 2),
        ],
        compiler_params=pltpu.CompilerParams(
            collective_id=0, has_side_effects=True, vmem_limit_bytes=60 << 20),
        name="divergence_grad",
    )(student_hidden, teacher_hidden, loss_weight.reshape(1, rows), student_head, teacher_head)
    return grad, loss.reshape(())


def divergence_terms(student_logits, teacher_logits, weights):
    differences = teacher_logits - student_logits
    peak_student, peak_teacher = lax.pmax(
        (jnp.max(student_logits, axis=1), jnp.max(teacher_logits, axis=1)), "voc"
    )
    scaled_student = jnp.exp(student_logits - peak_student[:, None])
    scaled_teacher = jnp.exp(teacher_logits - peak_teacher[:, None])
    total_student, total_teacher, cross_sum = lax.psum(
        (
            jnp.sum(scaled_student, axis=1),
            jnp.sum(scaled_teacher, axis=1),
            jnp.sum(scaled_teacher * differences, axis=1),
        ),
        "voc",
    )
    student_lse = peak_student + jnp.log(total_student)
    teacher_lse = peak_teacher + jnp.log(total_teacher)
    divergence = cross_sum / total_teacher - teacher_lse + student_lse
    prob_gap = jnp.exp(student_logits - student_lse[:, None]) - jnp.exp(
        teacher_logits - teacher_lse[:, None]
    )
    scaled_gap = (weights[:, None] * prob_gap).astype(jnp.bfloat16)
    return (divergence, scaled_gap)


def plain_shards(student_hidden, teacher_hidden, student_head, teacher_head, loss_weight):
    student_block, teacher_block = (
        lax.all_gather(student_hidden, "voc", axis=1, tiled=True),
        lax.all_gather(teacher_hidden, "voc", axis=1, tiled=True),
    )
    vocab_local = student_head.shape[1]
    row_count = student_block.shape[0] // lax.axis_size("hid")
    joined = lax.psum_scatter(
        jnp.concatenate(
            [
                jnp.dot(student_block, student_head, preferred_element_type=jnp.float32),
                jnp.dot(teacher_block, teacher_head, preferred_element_type=jnp.float32),
            ],
            axis=1,
        ),
        "hid",
        scatter_dimension=0,
        tiled=True,
    )
    student_logits = joined[:, :vocab_local]
    teacher_logits = joined[:, vocab_local:]
    weights = lax.dynamic_slice_in_dim(loss_weight, lax.axis_index("hid") * row_count, row_count)
    divergence, scaled_gap = divergence_terms(student_logits, teacher_logits, weights)
    token_total = loss_weight.shape[0] * lax.axis_size("tok")
    loss_total = lax.psum(jnp.sum(divergence), ("tok", "hid"))
    grad_terms = lax.dot_general(
        lax.all_gather(scaled_gap, "hid", axis=0, tiled=True),
        student_head,
        (((1,), (1,)), ((), ())),
        preferred_element_type=jnp.float32,
    )
    grad_hidden = lax.psum_scatter(grad_terms, "voc", scatter_dimension=1, tiled=True).astype(
        jnp.bfloat16
    )
    mean_loss = loss_total / token_total
    return (grad_hidden, mean_loss)


def solution(mesh):
    placed = (
        P("tok", ("hid", "voc")),
        P("tok", ("hid", "voc")),
        P("hid", "voc"),
        P("hid", "voc"),
        P("tok"),
    )
    n, nt = mesh.shape["voc"], mesh.shape["tok"]
    if 2 < n <= 4 and mesh.shape["hid"] == 2:
        body = functools.partial(fused_shards, n, nt)
    else:
        body = plain_shards
    return jax.shard_map(
        body,
        mesh=mesh,
        in_specs=placed,
        out_specs=(P("tok", ("hid", "voc")), P()),
        check_vma=False,
    )
```

profile of v0, /device:TPU:1, one launch (start us, length us, event | category | flops | bytes accessed | tf_op | source)
XLA Modules:
  0.0 82.7 jit_solution(603979957513369897)
XLA Ops:
  0.6 78.7 %divergence_grad.1 = (bf16[128,1024]{1,0:T(8,128)(2,1)}, f32[1,1]{1,0:T(1,128)}) custom-call(bf16[128,1024]{1,0:T(8,128)(2,1)} %x_hbm.1, bf16[128,2048]{1,0:T(8,128)(2,1)} %y_hbm.1, f32[1,128]{1,0:T(1,128)} %bitcast.2, bf16[4096,512]{1,0:T(8,128)(2,1)} %sw_hbm.1, bf16[8192,512]{1,0:T(8,128)(2,1)} %tw_hbm.1), custom_call_target="tpu_custom_call" | custom-call | tf_op jit(solution)/shard_map/divergence_grad/pallas_call | solution.py:342
  79.3 1.7 %copy.9 = bf16[128,1024]{1,0:T(8,128)(2,1)} copy(bf16[128,1024]{1,0:T(8,128)(2,1)} %get-tuple-element.8) | data formatting | bytes 524288
where the time goes:
time: 82.9 us; the launch traced here: 82.7 us
  Pallas kernels  78.7 us (95%)
  between operations  2.4 us (3%)
  local copies, waits for them, and re-layouts  1.67 us (2%)
    pallas_call x1, Pallas kernels, fused_shards(): pl.pallas_call(functools.partial(fused, n, nt), out_shape=(jax.ShapeDtype...  78.7 us
    unnamed x1, local copies, waits for them, and re-layouts  1.67 us

commit v1 on v0

v1 whole, which is shorter than its diff:
```python
import functools

import jax
import jax.numpy as jnp
from jax import lax
from jax.experimental import pallas as pl
from jax.experimental.pallas import tpu as pltpu
from jax.sharding import PartitionSpec as P

MESH = pl.DeviceIdType.MESH
F32 = jnp.float32
BF16 = jnp.bfloat16
GROUPS = 2


def fused(n, nt, ng, x_hbm, y_hbm, w_hbm, sw_hbm, tw_hbm, out, loss_out,
          x_ref, y_ref, w_ref, wf, tw, tg, sp, spx, ssum, srr, tacc, tpx, stat, gap, wcol, lossb, lossr, lossx, acc,
          lc, wz_s, wz_r, wt_s, wt_r, th_s, th_r, px_s, px_r, tx_s, tx_r, rs_s, rs_r,
          st_s, st_r, gz_s, gz_r, gx_s, gx_r, ls_s, ls_r):
    z = lax.axis_index("voc")
    t = lax.axis_index("tok")
    h = lax.axis_index("hid")
    rows, ks = x_ref.shape
    kt = y_ref.shape[1]
    half = rows // 2
    q = half // ng
    quarter = ks // nt
    eighth = quarter // 2
    partner = {"hid": 1 - h}
    mine = pl.ds(pl.multiple_of(h * half, half), half)
    theirs = pl.ds(pl.multiple_of((1 - h) * half, half), half)
    nbr = (t + 1 - 2 * lax.rem(t, 2), lax.rem(t + 2, 4))
    diag = nt - 1 - t
    at_end = jnp.logical_or(z == 0, z == n - 1)
    inside = jnp.logical_not(at_end)
    side_in = jnp.where(z < n // 2, 1, 0)
    side_out = 1 - side_in
    step_in = 2 * side_in - 1
    near, mid, far = z + step_in, z + 2 * step_in, z + 3 * step_in
    inner, beyond, outer = z + step_in, z + 2 * step_in, z - step_in

    def rc(src, dst, ss, rs, dev):
        return pltpu.make_async_remote_copy(
            src_ref=src, dst_ref=dst, send_sem=ss, recv_sem=rs,
            device_id=dev, device_id_type=MESH)

    def zdev(k):
        return lax.rem(z + k, n)

    def group(c, g):
        return pl.ds(pl.multiple_of(c * half + g * q, q), q)

    own_w = pltpu.make_async_copy(sw_hbm.at[pl.ds(pl.multiple_of(z * ks, ks), ks)], wf.at[z], lc.at[n])
    own_w.start()
    ins = [pltpu.make_async_copy(a, b, lc.at[n + 1 + i])
           for i, (a, b) in enumerate(((x_hbm, x_ref), (y_hbm, y_ref), (w_hbm, w_ref)))]
    for c in ins:
        c.start()

    def tw_copy(i):
        return pltpu.make_async_copy(tw_hbm.at[pl.ds(pl.multiple_of(i * kt, kt), kt)], tw.at[i], lc.at[i])

    barrier = pltpu.get_barrier_semaphore()
    for k in range(1, n):
        pl.semaphore_signal(barrier, inc=1, device_id={"voc": zdev(k)}, device_id_type=MESH)
    for k in range(1, nt):
        pl.semaphore_signal(barrier, inc=1, device_id={"tok": lax.rem(t + k, nt)}, device_id_type=MESH)
    pl.semaphore_signal(barrier, inc=1, device_id=partner, device_id_type=MESH)
    pl.semaphore_wait(barrier, n - 1 + nt - 1 + 1)

    def part(i):
        return pl.ds(pl.multiple_of(i * quarter, quarter), quarter)

    def subpart(i, b):
        return pl.ds(pl.multiple_of(i * quarter + b * eighth, eighth), eighth)

    def wz(j):
        return rc(sw_hbm.at[pl.ds(pl.multiple_of(j * ks + t * quarter, quarter), quarter)],
                  wf.at[z, part(t)], wz_s.at[j], wz_r.at[z], {"voc": j})

    def wz_in(j):
        return rc(wf.at[j, part(t)], wf.at[j, part(t)], wz_s.at[j], wz_r.at[j], {"voc": j})

    def wt(j, k):
        return rc(wf.at[j, part(t)], wf.at[j, part(t)], wt_s.at[j, k], wt_r.at[j, k], {"tok": nbr[k]})

    def wt_in(j, k):
        return rc(wf.at[j, part(nbr[k])], wf.at[j, part(nbr[k])], wt_s.at[j, k], wt_r.at[j, k], {"tok": nbr[k]})

    def wd(j, k):
        piece = wf.at[j, subpart(nbr[k], k)]
        return rc(piece, piece, wt_s.at[j, 2 + k], wt_r.at[j, 2 + k], {"tok": nbr[1 - k]})

    def wd_in(j, k):
        piece = wf.at[j, subpart(diag, k)]
        return rc(piece, piece, wt_s.at[j, 2 + k], wt_r.at[j, 2 + k], {"tok": nbr[1 - k]})

    def y_send(src, i, g, c, k, dev):
        return rc(src.at[group(c, g)], tg.at[i, group(c, g)], th_s.at[k, 2 * g + c], th_r.at[i, 2 * g + c], {"voc": dev})

    def y_own(g, c, k, dev):
        return y_send(y_hbm, z, g, c, k, dev)

    def y_relay(i, g, c, k):
        return y_send(tg.at[i], i, g, c, k, outer)

    def y_out(g, k, dev, cs=(0, 1)):
        for c in cs:
            y_own(g, c, k, dev).start()

    @pl.when(at_end)
    def _():
        for j in (near, mid, far):
            wz(j).start()
        y_out(0, 0, near)

    @pl.when(inside)
    def _():
        for j in (outer, inner, beyond):
            wz(j).start()
        y_out(0, 1, outer)
        y_out(0, 0, inner)
        for g in range(1, ng):
            y_out(g, 1, outer)
            y_out(g, 0, inner)

    for k in range(n):
        tw_copy(zdev(k)).start()

    for c in ins:
        c.wait()
    wcol[...] = jnp.transpose(jnp.broadcast_to(w_ref[...], (rows, rows)))

    def w_arrive(j):
        wz_in(j).wait_recv()
        for k in range(2):
            wt(j, k).start()

    def w_spread(j):
        for k in range(2):
            wt_in(j, k).wait_recv()
            wd(j, k).start()

    def teacher_dot(src, i, g, first):
        step = kt // 2

        @pl.loop(0, 2)
        def _(s):
            cols = pl.ds(pl.multiple_of(s * step, step), step)
            both = jnp.concatenate([src[pl.ds(c * half + g * q, q), cols] for c in range(2)], axis=0)
            term = jnp.dot(both, tw[i, cols, :], preferred_element_type=F32)
            if first:
                @pl.when(s == 0)
                def _():
                    tacc[g] = term

                @pl.when(s > 0)
                def _():
                    tacc[g] += term
            else:
                tacc[g] += term

    def take_y(i, g, c, k=None):
        y_send(tg.at[i], i, g, c, 0, outer).wait_recv()
        if k is not None:
            y_relay(i, g, c, k).start()

    def dot_y(i, g):
        teacher_dot(tg.at[i], i, g, False)

    def full_y(i, g, k=None):
        for c in range(2):
            take_y(i, g, c, k)
        dot_y(i, g)

    def student(j):
        sp[j] = jnp.dot(x_ref[...], wf[j], preferred_element_type=F32)
        rc(sp.at[j, theirs], spx.at[j], px_s.at[j], px_r.at[j], partner).start()

    def student_sum(j):
        rc(sp.at[j, theirs], spx.at[j], px_s.at[j], px_r.at[j], partner).wait_recv()
        ssum[j] = sp[j, mine, :] + spx[j]

    def rs(side, j):
        return rc(ssum.at[j], srr.at[side, j], rs_s.at[j], rs_r.at[side, j], {"voc": z + 2 * side - 1})

    def student_full(j):
        for k in range(2):
            wd_in(j, k).wait_recv()
        student(j)

    def rs_take(side, j):
        rs(side, j).wait_recv()
        ssum[j] += srr[side, j]

    def student_pass(j, side, upstream):
        student_sum(j)
        if upstream:
            rs_take(side, j)
        rs(side, j).start()

    def t_swap(g):
        return rc(tacc.at[g, pl.ds(pl.multiple_of((1 - h) * q, q), q)], tpx.at[g], tx_s.at[g], tx_r.at[g], partner)

    def stx(g, j, src):
        return rc(stat.at[g, src], stat.at[g, src], st_s.at[g, j], st_r.at[g, src], {"voc": j})

    def gz(g, j, src):
        return rc(gap.at[src, group(h, g)], gap.at[src, group(h, g)], gz_s.at[g, j], gz_r.at[g, src], {"voc": j})

    def gx(g, src, c):
        return rc(gap.at[src, group(c, g)], gap.at[src, group(c, g)], gx_s.at[g, src], gx_r.at[g, src], partner)

    def send_stats(g):
        t_swap(g).wait_recv()
        tl = tacc[g, pl.ds(pl.multiple_of(h * q, q), q), :] + tpx[g]
        tpx[g] = tl
        sl = ssum[z, pl.ds(g * q, q), :]
        ms = jnp.max(sl, axis=1, keepdims=True)
        ss = jnp.sum(jnp.exp(sl - ms), axis=1, keepdims=True)
        mt = jnp.max(tl, axis=1, keepdims=True)
        et = jnp.exp(tl - mt)
        st = jnp.sum(et, axis=1, keepdims=True)
        cr = jnp.sum(et * (tl - sl), axis=1, keepdims=True)
        lane = lax.broadcasted_iota(jnp.int32, (q, 128), 1)
        cols = jnp.where(lane == 0, ms, jnp.where(lane == 1, mt, jnp.where(
            lane == 2, ss, jnp.where(lane == 3, st, cr))))
        stat[g, z] = jnp.transpose(jnp.concatenate([cols] * (128 // q), axis=0))[:8]
        for k in (2, 1, 3):
            stx(g, zdev(k), z).start()

    def send_gap(g):
        for k in range(1, n):
            stx(g, zdev(k), zdev(k)).wait_recv()
        parts = [stat[g, j] for j in range(n)]
        top = parts[0]
        for p in parts[1:]:
            top = jnp.maximum(top, p)
        big_s, big_t = top[0:1], top[1:2]
        tot_s = jnp.zeros_like(big_s)
        tot_t = jnp.zeros_like(big_s)
        cross = jnp.zeros_like(big_s)
        for p in parts:
            es = jnp.exp(p[0:1] - big_s)
            ets = jnp.exp(p[1:2] - big_t)
            tot_s = tot_s + p[2:3] * es
            tot_t = tot_t + p[3:4] * ets
            cross = cross + p[4:5] * ets
        lse_s = big_s + jnp.log(tot_s)
        lse_t = big_t + jnp.log(tot_t)
        scale = wcol[group(h, g), :][:, 0:1]
        sub = lax.broadcasted_iota(jnp.int32, (128, 128), 0)
        back = jnp.transpose(jnp.where(sub == 0, lse_s, lse_t))[:q]
        col_s, col_t = back[:, 0:1], back[:, 1:2]
        sl = ssum[z, pl.ds(g * q, q), :]
        gap[z, group(h, g), :] = (scale * (jnp.exp(sl - col_s) - jnp.exp(tpx[g] - col_t))).astype(BF16)
        for k in (2, 1, 3):
            gz(g, zdev(k), z).start()
        gx(g, z, h).start()
        div = cross / tot_t - lse_t + lse_s
        first = lax.broadcasted_iota(jnp.int32, div.shape, 1) < q
        lossr[g] = jnp.broadcast_to(jnp.sum(jnp.where(first, div, 0.0), axis=1, keepdims=True), (8, 128))

    def take_gap(g, j):
        gz(g, j, j).wait_recv()
        gx(g, j, h).start()

    def grad_dot(g, j, first):
        gx(g, j, 1 - h).wait_recv()
        both = jnp.concatenate([gap[j, pl.ds(c * half + g * q, q), :] for c in range(2)], axis=0)
        term = lax.dot_general(both, wf[j], (((1,), (1,)), ((), ())), preferred_element_type=F32)
        if first:
            acc[g] = term
        else:
            acc[g] += term

    def store(g):
        for c in range(2):
            out[pl.ds(c * half + g * q, q), :] = acc[g, pl.ds(c * q, q), :].astype(BF16)

    def local_dots():
        for i in range(n):
            tw_copy(i).wait()
        for g in range(ng):
            teacher_dot(y_ref, z, g, True)
        own_w.wait()
        student(z)

    @pl.when(at_end)
    def _():
        w_arrive(near)
        local_dots()
        w_spread(near)
        student_full(near)
        w_arrive(far)
        w_spread(far)
        y_out(0, 1, mid)
        student_pass(near, side_in, False)
        w_arrive(mid)
        student_full(far)
        full_y(near, 0)
        student_pass(far, side_in, False)
        w_spread(mid)
        full_y(near, 1)
        student_full(mid)

        @pl.when(h == 1)
        def _():
            y_out(1, 1, mid)
        student_sum(z)
        student_pass(mid, side_in, False)

        @pl.when(h == 0)
        def _():
            y_out(1, 1, mid)
        y_out(1, 0, near)
        full_y(far, 0)
        full_y(mid, 0)
        t_swap(0).start()
        full_y(mid, 1)
        rs_take(side_out, z)
        send_stats(0)
        full_y(far, 1)
        t_swap(1).start()

    @pl.when(inside)
    def _():
        w_arrive(outer)
        local_dots()
        w_spread(outer)
        w_arrive(inner)
        w_arrive(beyond)
        student_full(outer)
        w_spread(inner)
        w_spread(beyond)
        take_y(inner, 0, 0, 3)
        take_y(beyond, 0, 0, 2)
        student_full(inner)
        take_y(inner, 0, 1, 3)
        take_y(beyond, 0, 1, 2)
        full_y(outer, 0)
        student_full(beyond)
        dot_y(beyond, 0)
        student_pass(beyond, side_in, True)
        dot_y(inner, 0)
        t_swap(0).start()
        take_y(inner, 1, 0, 3)
        take_y(inner, 1, 1, 3)
        student_pass(outer, side_out, True)
        dot_y(inner, 1)
        take_y(beyond, 1, 0, 2)
        take_y(beyond, 1, 1, 2)
        student_pass(inner, side_in, True)
        dot_y(beyond, 1)
        student_sum(z)
        rs_take(side_in, z)
        rs_take(side_out, z)
        send_stats(0)
        full_y(outer, 1)
        t_swap(1).start()

    def lp():
        return rc(lossb.at[0], lossb.at[1], ls_s.at[nt], ls_r.at[nt], partner)

    def ls(a, b):
        return rc(lossx.at[b], lossx.at[b], ls_s.at[a], ls_r.at[b], {"tok": a})

    send_stats(1)
    send_gap(0)
    send_gap(1)
    lossb[0] = lossr[0] + lossr[1]
    lp().start()
    across = lax.rem(z + 2, n)
    order = (near, across, n * (n - 1) // 2 - z - near - across)
    grad_dot(0, z, True)
    for j in order:
        take_gap(0, j)
    lp().wait_recv()
    lossx[t] = lossb[0] + lossb[1]
    for k in range(1, nt):
        ls(lax.rem(t + k, nt), t).start()
    grad_dot(1, z, True)
    for j in order:
        grad_dot(0, j, False)
    store(0)
    for j in order:
        take_gap(1, j)
    for j in order:
        grad_dot(1, j, False)
    store(1)
    for k in range(1, nt):
        ls(t, lax.rem(t + k, nt)).wait_recv()
    total = lossx[0]
    for a in range(1, nt):
        total = total + lossx[a]
    loss_out[0, 0] = total[0, 0] / (rows * nt)

    for k in range(1, n):
        j = zdev(k)
        wz(j).wait_send()
        for b in range(2):
            wt(j, b).wait_send()
            wd(j, b).wait_send()
        rs(side_in, j).wait_send()
    for g in range(ng):
        for k in range(1, n):
            stx(g, zdev(k), z).wait_send()
            gz(g, zdev(k), z).wait_send()
        for c in range(2):
            y_own(g, c, 0, near).wait_send()

            @pl.when(at_end)
            def _(g=g, c=c):
                y_own(g, c, 1, mid).wait_send()

            @pl.when(inside)
            def _(g=g, c=c):
                y_own(g, c, 1, outer).wait_send()
                for k, j in ((2, beyond), (3, inner)):
                    y_relay(j, g, c, k).wait_send()
        for j in range(n):
            gx(g, j, h).wait_send()
        t_swap(g).wait_send()
    for j in range(n):
        rc(sp.at[j, theirs], spx.at[j], px_s.at[j], px_r.at[j], partner).wait_send()
    lp().wait_send()
    for k in range(1, nt):
        ls(lax.rem(t + k, nt), t).wait_send()


def fused_shards(n, nt, student_hidden, teacher_hidden, student_head, teacher_head, loss_weight):
    rows, ks = student_hidden.shape
    kt = teacher_hidden.shape[1]
    v = student_head.shape[1]
    half = rows // 2
    ng = GROUPS
    q = half // ng
    dma = lambda *s: pltpu.SemaphoreType.DMA(s)
    vmem = lambda s, d: pltpu.VMEM(s, d)
    whole = pl.BlockSpec(memory_space=pltpu.VMEM)
    anywhere = pl.BlockSpec(memory_space=pl.ANY)
    grad, loss = pl.pallas_call(
        functools.partial(fused, n, nt, ng),
        out_shape=(jax.ShapeDtypeStruct((rows, ks), BF16), jax.ShapeDtypeStruct((1, 1), F32)),
        in_specs=[anywhere] * 5,
        out_specs=(whole, pl.BlockSpec(memory_space=pltpu.SMEM)),
        scratch_shapes=[
            vmem((rows, ks), BF16),
            vmem((rows, kt), BF16),
            vmem((1, rows), F32),
            vmem((n, ks, v), BF16),
            vmem((n, kt, v), BF16),
            vmem((n, rows, kt), BF16),
            vmem((n, rows, v), F32),
            vmem((n, half, v), F32),
            vmem((n, half, v), F32),
            vmem((2, n, half, v), F32),
            vmem((ng, 2 * q, v), F32),
            vmem((ng, q, v), F32),
            vmem((ng, n, 8, 128), F32),
            vmem((n, rows, v), BF16),
            vmem((rows, rows), F32),
            vmem((2, 8, 128), F32),
            vmem((ng, 8, 128), F32),
            vmem((nt, 8, 128), F32),
            vmem((ng, 2 * q, ks), F32),
            dma(n + 4),
            dma(n), dma(n), dma(n, 4), dma(n, 4),
            dma(4, 2 * ng), dma(n, 2 * ng),
            dma(n), dma(n), dma(ng), dma(ng), dma(n), dma(2, n),
            dma(ng, n), dma(ng, n), dma(ng, n), dma(ng, n), dma(ng, n), dma(ng, n),
            dma(nt + 1), dma(nt + 1),
        ],
        compiler_params=pltpu.CompilerParams(
            collective_id=0, has_side_effects=True, vmem_limit_bytes=60 << 20),
        name="divergence_grad",
    )(student_hidden, teacher_hidden, loss_weight.reshape(1, rows), student_head, teacher_head)
    return grad, loss.reshape(())


def divergence_terms(student_logits, teacher_logits, weights):
    differences = teacher_logits - student_logits
    peak_student, peak_teacher = lax.pmax(
        (jnp.max(student_logits, axis=1), jnp.max(teacher_logits, axis=1)), "voc"
    )
    scaled_student = jnp.exp(student_logits - peak_student[:, None])
    scaled_teacher = jnp.exp(teacher_logits - peak_teacher[:, None])
    total_student, total_teacher, cross_sum = lax.psum(
        (
            jnp.sum(scaled_student, axis=1),
            jnp.sum(scaled_teacher, axis=1),
            jnp.sum(scaled_teacher * differences, axis=1),
        ),
        "voc",
    )
    student_lse = peak_student + jnp.log(total_student)
    teacher_lse = peak_teacher + jnp.log(total_teacher)
    divergence = cross_sum / total_teacher - teacher_lse + student_lse
    prob_gap = jnp.exp(student_logits - student_lse[:, None]) - jnp.exp(
        teacher_logits - teacher_lse[:, None]
    )
    scaled_gap = (weights[:, None] * prob_gap).astype(jnp.bfloat16)
    return (divergence, scaled_gap)


def plain_shards(student_hidden, teacher_hidden, student_head, teacher_head, loss_weight):
    student_block, teacher_block = (
        lax.all_gather(student_hidden, "voc", axis=1, tiled=True),
        lax.all_gather(teacher_hidden, "voc", axis=1, tiled=True),
    )
    vocab_local = student_head.shape[1]
    row_count = student_block.shape[0] // lax.axis_size("hid")
    joined = lax.psum_scatter(
        jnp.concatenate(
            [
                jnp.dot(student_block, student_head, preferred_element_type=jnp.float32),
                jnp.dot(teacher_block, teacher_head, preferred_element_type=jnp.float32),
            ],
            axis=1,
        ),
        "hid",
        scatter_dimension=0,
        tiled=True,
    )
    student_logits = joined[:, :vocab_local]
    teacher_logits = joined[:, vocab_local:]
    weights = lax.dynamic_slice_in_dim(loss_weight, lax.axis_index("hid") * row_count, row_count)
    divergence, scaled_gap = divergence_terms(student_logits, teacher_logits, weights)
    token_total = loss_weight.shape[0] * lax.axis_size("tok")
    loss_total = lax.psum(jnp.sum(divergence), ("tok", "hid"))
    grad_terms = lax.dot_general(
        lax.all_gather(scaled_gap, "hid", axis=0, tiled=True),
        student_head,
        (((1,), (1,)), ((), ())),
        preferred_element_type=jnp.float32,
    )
    grad_hidden = lax.psum_scatter(grad_terms, "voc", scatter_dimension=1, tiled=True).astype(
        jnp.bfloat16
    )
    mean_loss = loss_total / token_total
    return (grad_hidden, mean_loss)


def solution(mesh):
    placed = (
        P("tok", ("hid", "voc")),
        P("tok", ("hid", "voc")),
        P("hid", "voc"),
        P("hid", "voc"),
        P("tok"),
    )
    n, nt = mesh.shape["voc"], mesh.shape["tok"]
    if n == 4 and nt == 4 and mesh.shape["hid"] == 2:
        body = functools.partial(fused_shards, n, nt)
    else:
        body = plain_shards
    return jax.shard_map(
        body,
        mesh=mesh,
        in_specs=placed,
        out_specs=(P("tok", ("hid", "voc")), P()),
        check_vma=False,
    )
```

time: 82.9 us -> 81.3 us (0.981)
  Pallas kernels: 78.7 us -> 77 us
    pallas_call x1, Pallas kernels: 78.7 us -> 77 us  [fused_shards(): pl.pallas_call(functools.partial(fused, n, nt, ng), out_shape=(jax.ShapeD...]
where the time goes in v1:
time: 81.3 us; the launch traced here: 81.1 us
  Pallas kernels  77 us (95%)
  between operations  2.4 us (3%)
  local copies, waits for them, and re-layouts  1.67 us (2%)
    pallas_call x1, Pallas kernels, fused_shards(): pl.pallas_call(functools.partial(fused, n, nt, ng), out_shape=(jax.ShapeD...  77 us
    unnamed x1, local copies, waits for them, and re-layouts  1.67 us

profile of v1, /device:TPU:1, one launch (start us, length us, event | category | flops | bytes accessed | tf_op | source)
XLA Modules:
  0.0 81.1 jit_solution(17332945548095117179)
XLA Ops:
  0.6 77.0 %divergence_grad.1 = (bf16[128,1024]{1,0:T(8,128)(2,1)}, f32[1,1]{1,0:T(1,128)}) custom-call(bf16[128,1024]{1,0:T(8,128)(2,1)} %x_hbm.1, bf16[128,2048]{1,0:T(8,128)(2,1)} %y_hbm.1, f32[1,128]{1,0:T(1,128)} %bitcast.2, bf16[4096,512]{1,0:T(8,128)(2,1)} %sw_hbm.1, bf16[8192,512]{1,0:T(8,128)(2,1)} %tw_hbm.1), custom_call_target="tpu_custom_call" | custom-call | tf_op jit(solution)/shard_map/divergence_grad/pallas_call | solution.py:442
  77.7 1.7 %copy.9 = bf16[128,1024]{1,0:T(8,128)(2,1)} copy(bf16[128,1024]{1,0:T(8,128)(2,1)} %get-tuple-element.8) | data formatting | bytes 524288

commit v2 on v1

--- a/solution.py
+++ b/solution.py
@@ -14,9 +14,9 @@
 
 
 def fused(n, nt, ng, x_hbm, y_hbm, w_hbm, sw_hbm, tw_hbm, out, loss_out,
-          x_ref, y_ref, w_ref, wf, tw, tg, sp, spx, ssum, srr, tacc, tpx, stat, gap, wcol, lossb, lossr, lossx, acc,
+          x_ref, y_ref, w_ref, wf, tw, tg, sp, spx, ssum, srr, tacc, tpx, stat, gap, wcol, lossb, lossr, lossx, acc, stage,
           lc, wz_s, wz_r, wt_s, wt_r, th_s, th_r, px_s, px_r, tx_s, tx_r, rs_s, rs_r,
-          st_s, st_r, gz_s, gz_r, gx_s, gx_r, ls_s, ls_r):
+          st_s, st_r, gz_s, gz_r, gx_s, gx_r, ls_s, ls_r, oc):
     z = lax.axis_index("voc")
     t = lax.axis_index("tok")
     h = lax.axis_index("hid")
@@ -274,9 +274,39 @@
         else:
             acc[g] += term
 
+    def out_copy(g, c):
+        rows_gc = pl.ds(c * half + g * q, q)
+        return pltpu.make_async_copy(stage.at[rows_gc], out.at[rows_gc], oc.at[2 * g + c])
+
     def store(g):
         for c in range(2):
-            out[pl.ds(c * half + g * q, q), :] = acc[g, pl.ds(c * q, q), :].astype(BF16)
+            stage[pl.ds(c * half + g * q, q), :] = acc[g, pl.ds(c * q, q), :].astype(BF16)
+            out_copy(g, c).start()
+
+    def drain_bulk():
+        for k in range(1, n):
+            j = zdev(k)
+            wz(j).wait_send()
+            for b in range(2):
+                wt(j, b).wait_send()
+                wd(j, b).wait_send()
+            rs(side_in, j).wait_send()
+        for g in range(ng):
+            for c in range(2):
+                y_own(g, c, 0, near).wait_send()
+
+                @pl.when(at_end)
+                def _(g=g, c=c):
+                    y_own(g, c, 1, mid).wait_send()
+
+                @pl.when(inside)
+                def _(g=g, c=c):
+                    y_own(g, c, 1, outer).wait_send()
+                    for k, j in ((2, beyond), (3, inner)):
+                        y_relay(j, g, c, k).wait_send()
+            t_swap(g).wait_send()
+        for j in range(n):
+            rc(sp.at[j, theirs], spx.at[j], px_s.at[j], px_r.at[j], partner).wait_send()
 
     def local_dots():
         for i in range(n):
@@ -336,21 +366,31 @@
         take_y(inner, 0, 0, 3)
         take_y(beyond, 0, 0, 2)
         student_full(inner)
+        take_y(beyond, 0, 1, 2)
+        dot_y(beyond, 0)
+        full_y(outer, 0)
         take_y(inner, 0, 1, 3)
-        take_y(beyond, 0, 1, 2)
-        full_y(outer, 0)
         student_full(beyond)
-        dot_y(beyond, 0)
         student_pass(beyond, side_in, True)
         dot_y(inner, 0)
         t_swap(0).start()
         take_y(inner, 1, 0, 3)
         take_y(inner, 1, 1, 3)
-        student_pass(outer, side_out, True)
+
+        @pl.when(h == 1)
+        def _():
+            take_y(beyond, 1, 0, 2)
+            take_y(beyond, 1, 1, 2)
+            student_pass(outer, side_out, True)
+            student_pass(inner, side_in, True)
+
+        @pl.when(h == 0)
+        def _():
+            student_pass(outer, side_out, True)
+            take_y(beyond, 1, 0, 2)
+            student_pass(inner, side_in, True)
+            take_y(beyond, 1, 1, 2)
         dot_y(inner, 1)
-        take_y(beyond, 1, 0, 2)
-        take_y(beyond, 1, 1, 2)
-        student_pass(inner, side_in, True)
         dot_y(beyond, 1)
         student_sum(z)
         rs_take(side_in, z)
@@ -367,6 +407,7 @@
 
     send_stats(1)
     send_gap(0)
+    drain_bulk()
     send_gap(1)
     lossb[0] = lossr[0] + lossr[1]
     lp().start()
@@ -395,37 +436,18 @@
         total = total + lossx[a]
     loss_out[0, 0] = total[0, 0] / (rows * nt)
 
-    for k in range(1, n):
-        j = zdev(k)
-        wz(j).wait_send()
-        for b in range(2):
-            wt(j, b).wait_send()
-            wd(j, b).wait_send()
-        rs(side_in, j).wait_send()
     for g in range(ng):
         for k in range(1, n):
             stx(g, zdev(k), z).wait_send()
             gz(g, zdev(k), z).wait_send()
-        for c in range(2):
-            y_own(g, c, 0, near).wait_send()
-
-            @pl.when(at_end)
-            def _(g=g, c=c):
-                y_own(g, c, 1, mid).wait_send()
-
-            @pl.when(inside)
-            def _(g=g, c=c):
-                y_own(g, c, 1, outer).wait_send()
-                for k, j in ((2, beyond), (3, inner)):
-                    y_relay(j, g, c, k).wait_send()
         for j in range(n):
             gx(g, j, h).wait_send()
-        t_swap(g).wait_send()
-    for j in range(n):
-        rc(sp.at[j, theirs], spx.at[j], px_s.at[j], px_r.at[j], partner).wait_send()
     lp().wait_send()
     for k in range(1, nt):
         ls(lax.rem(t + k, nt), t).wait_send()
+    for g in range(ng):
+        for c in range(2):
+            out_copy(g, c).wait()
 
 
 def fused_shards(n, nt, student_hidden, teacher_hidden, student_head, teacher_head, loss_weight):
@@ -437,13 +459,12 @@
     q = half // ng
     dma = lambda *s: pltpu.SemaphoreType.DMA(s)
     vmem = lambda s, d: pltpu.VMEM(s, d)
-    whole = pl.BlockSpec(memory_space=pltpu.VMEM)
     anywhere = pl.BlockSpec(memory_space=pl.ANY)
     grad, loss = pl.pallas_call(
         functools.partial(fused, n, nt, ng),
         out_shape=(jax.ShapeDtypeStruct((rows, ks), BF16), jax.ShapeDtypeStruct((1, 1), F32)),
         in_specs=[anywhere] * 5,
-        out_specs=(whole, pl.BlockSpec(memory_space=pltpu.SMEM)),
+        out_specs=(anywhere, pl.BlockSpec(memory_space=pltpu.SMEM)),
         scratch_shapes=[
             vmem((rows, ks), BF16),
             vmem((rows, kt), BF16),
@@ -464,12 +485,13 @@
             vmem((ng, 8, 128), F32),
             vmem((nt, 8, 128), F32),
             vmem((ng, 2 * q, ks), F32),
+            vmem((rows, ks), BF16),
             dma(n + 4),
             dma(n), dma(n), dma(n, 4), dma(n, 4),
             dma(4, 2 * ng), dma(n, 2 * ng),
             dma(n), dma(n), dma(ng), dma(ng), dma(n), dma(2, n),
             dma(ng, n), dma(ng, n), dma(ng, n), dma(ng, n), dma(ng, n), dma(ng, n),
-            dma(nt + 1), dma(nt + 1),
+            dma(nt + 1), dma(nt + 1), dma(2 * ng),
         ],
         compiler_params=pltpu.CompilerParams(
             collective_id=0, has_side_effects=True, vmem_limit_bytes=60 << 20),

time: 81.3 us -> 80.2 us (0.986)
  Pallas kernels: 77 us -> 76 us
    pallas_call x1, Pallas kernels: 77 us -> 76 us  [fused_shards(): pl.pallas_call(functools.partial(fused, n, nt, ng), out_shape=(jax.ShapeD...]
where the time goes in v2:
time: 80.2 us; the launch traced here: 80 us
  Pallas kernels  76 us (95%)
  between operations  2.4 us (3%)
  local copies, waits for them, and re-layouts  1.67 us (2%)
    pallas_call x1, Pallas kernels, fused_shards(): pl.pallas_call(functools.partial(fused, n, nt, ng), out_shape=(jax.ShapeD...  76 us
    unnamed x1, local copies, waits for them, and re-layouts  1.67 us

profile of v2, /device:TPU:1, one launch (start us, length us, event | category | flops | bytes accessed | tf_op | source)
XLA Modules:
  0.0 80.0 jit_solution(12136548844091404983)
XLA Ops:
  0.6 76.0 %divergence_grad.1 = (bf16[128,1024]{1,0:T(8,128)(2,1)}, f32[1,1]{1,0:T(1,128)}) custom-call(bf16[128,1024]{1,0:T(8,128)(2,1)} %x_hbm.1, bf16[128,2048]{1,0:T(8,128)(2,1)} %y_hbm.1, f32[1,128]{1,0:T(1,128)} %bitcast.2, bf16[4096,512]{1,0:T(8,128)(2,1)} %sw_hbm.1, bf16[8192,512]{1,0:T(8,128)(2,1)} %tw_hbm.1), custom_call_target="tpu_custom_call" | custom-call | tf_op jit(solution)/shard_map/divergence_grad/pallas_call | solution.py:463
  76.6 1.7 %copy.9 = bf16[128,1024]{1,0:T(8,128)(2,1)} copy(bf16[128,1024]{1,0:T(8,128)(2,1)} %get-tuple-element.8) | data formatting | bytes 524288

commit v3 on v2

--- a/solution.py
+++ b/solution.py
@@ -14,9 +14,9 @@
 
 
 def fused(n, nt, ng, x_hbm, y_hbm, w_hbm, sw_hbm, tw_hbm, out, loss_out,
-          x_ref, y_ref, w_ref, wf, tw, tg, sp, spx, ssum, srr, tacc, tpx, stat, gap, wcol, lossb, lossr, lossx, acc, stage,
+          x_ref, y_ref, w_ref, wf, tw, tg, sp, spx, ssum, srr, tacc, tpx, stat, gap, wcol, lossb, lossr, lossx, acc,
           lc, wz_s, wz_r, wt_s, wt_r, th_s, th_r, px_s, px_r, tx_s, tx_r, rs_s, rs_r,
-          st_s, st_r, gz_s, gz_r, gx_s, gx_r, ls_s, ls_r, oc):
+          st_s, st_r, gz_s, gz_r, gx_s, gx_r, ls_s, ls_r):
     z = lax.axis_index("voc")
     t = lax.axis_index("tok")
     h = lax.axis_index("hid")
@@ -274,14 +274,9 @@
         else:
             acc[g] += term
 
-    def out_copy(g, c):
-        rows_gc = pl.ds(c * half + g * q, q)
-        return pltpu.make_async_copy(stage.at[rows_gc], out.at[rows_gc], oc.at[2 * g + c])
-
     def store(g):
         for c in range(2):
-            stage[pl.ds(c * half + g * q, q), :] = acc[g, pl.ds(c * q, q), :].astype(BF16)
-            out_copy(g, c).start()
+            out[pl.ds(c * half + g * q, q), :] = acc[g, pl.ds(c * q, q), :].astype(BF16)
 
     def drain_bulk():
         for k in range(1, n):
@@ -445,9 +440,6 @@
     lp().wait_send()
     for k in range(1, nt):
         ls(lax.rem(t + k, nt), t).wait_send()
-    for g in range(ng):
-        for c in range(2):
-            out_copy(g, c).wait()
 
 
 def fused_shards(n, nt, student_hidden, teacher_hidden, student_head, teacher_head, loss_weight):
@@ -462,9 +454,9 @@
     anywhere = pl.BlockSpec(memory_space=pl.ANY)
     grad, loss = pl.pallas_call(
         functools.partial(fused, n, nt, ng),
-        out_shape=(jax.ShapeDtypeStruct((rows, ks), BF16), jax.ShapeDtypeStruct((1, 1), F32)),
+        out_shape=(pltpu.VMEM((rows, ks), BF16), pltpu.SMEM((1, 1), F32)),
         in_specs=[anywhere] * 5,
-        out_specs=(anywhere, pl.BlockSpec(memory_space=pltpu.SMEM)),
+        out_specs=(pl.BlockSpec(memory_space=pltpu.VMEM), pl.BlockSpec(memory_space=pltpu.SMEM)),
         scratch_shapes=[
             vmem((rows, ks), BF16),
             vmem((rows, kt), BF16),
@@ -485,13 +477,12 @@
             vmem((ng, 8, 128), F32),
             vmem((nt, 8, 128), F32),
             vmem((ng, 2 * q, ks), F32),
-            vmem((rows, ks), BF16),
             dma(n + 4),
             dma(n), dma(n), dma(n, 4), dma(n, 4),
             dma(4, 2 * ng), dma(n, 2 * ng),
             dma(n), dma(n), dma(ng), dma(ng), dma(n), dma(2, n),
             dma(ng, n), dma(ng, n), dma(ng, n), dma(ng, n), dma(ng, n), dma(ng, n),
-            dma(nt + 1), dma(nt + 1), dma(2 * ng),
+            dma(nt + 1), dma(nt + 1),
         ],
         compiler_params=pltpu.CompilerParams(
             collective_id=0, has_side_effects=True, vmem_limit_bytes=60 << 20),

time: 80.2 us -> 76.8 us (0.958)
  between operations: 2.4 us -> 1.16 us
  Pallas kernels: 76 us -> 74.8 us
  local copies, waits for them, and re-layouts: 1.67 us -> 0.71 us
    pallas_call x1, Pallas kernels: 76 us -> 74.8 us  [fused_shards(): pl.pallas_call(functools.partial(fused, n, nt, ng), out_shape=(pltpu.VMEM...]
    unnamed x1, local copies, waits for them, and re-layouts: 1.67 us -> 0.71 us
where the time goes in v3:
time: 76.8 us; the launch traced here: 76.7 us
  Pallas kernels  74.8 us (97%)
  between operations  1.16 us (2%)
    pallas_call x1, Pallas kernels, fused_shards(): pl.pallas_call(functools.partial(fused, n, nt, ng), out_shape=(pltpu.VMEM...  74.8 us

profile of v3, /device:TPU:1, one launch (start us, length us, event | category | flops | bytes accessed | tf_op | source)
XLA Modules:
  0.0 76.7 jit_solution(18442590089270476925)
XLA Ops:
  0.6 74.8 %divergence_grad.1 = (bf16[128,1024]{1,0:T(8,128)(2,1)S(1)}, f32[1,1]{1,0:T(1,128)S(4)}) custom-call(bf16[128,1024]{1,0:T(8,128)(2,1)} %x_hbm.1, bf16[128,2048]{1,0:T(8,128)(2,1)} %y_hbm.1, f32[1,128]{1,0:T(1,128)} %bitcast.2, bf16[4096,512]{1,0:T(8,128)(2,1)} %sw_hbm.1, bf16[8192,512]{1,0:T(8,128)(2,1)} %tw_hbm.1), custom_call_target="tpu_custom_call" | custom-call | tf_op jit(solution)/shard_map/divergence_grad/pallas_call | solution.py:455
  76.0 0.7 copy.9

commit v4 on v3

--- a/solution.py
+++ b/solution.py
@@ -95,8 +95,11 @@
         piece = wf.at[j, subpart(diag, k)]
         return rc(piece, piece, wt_s.at[j, 2 + k], wt_r.at[j, 2 + k], {"tok": nbr[1 - k]})
 
+    owner = (1 - h, h)
+
     def y_send(src, i, g, c, k, dev):
-        return rc(src.at[group(c, g)], tg.at[i, group(c, g)], th_s.at[k, 2 * g + c], th_r.at[i, 2 * g + c], {"voc": dev})
+        rows_gc = group(owner[c], g)
+        return rc(src.at[rows_gc], tg.at[i, rows_gc], th_s.at[k, 2 * g + c], th_r.at[i, 2 * g + c], {"voc": dev})
 
     def y_own(g, c, k, dev):
         return y_send(y_hbm, z, g, c, k, dev)
@@ -167,6 +170,20 @@
 
     def dot_y(i, g):
         teacher_dot(tg.at[i], i, g, False)
+
+    def split_y(i, g):
+        step = kt // 2
+        for c in range(2):
+            take_y(i, g, c)
+            mine_gc = pl.ds(pl.multiple_of(owner[c] * q, q), q)
+
+            @pl.loop(0, 2)
+            def _(s):
+                cols = pl.ds(pl.multiple_of(s * step, step), step)
+                term = jnp.dot(tg[i, group(owner[c], g), cols], tw[i, cols, :], preferred_element_type=F32)
+                tacc[g, mine_gc, :] += term
+            if c == 0:
+                t_swap(g).start()
 
     def full_y(i, g, k=None):
         for c in range(2):
@@ -345,8 +362,7 @@
         full_y(mid, 1)
         rs_take(side_out, z)
         send_stats(0)
-        full_y(far, 1)
-        t_swap(1).start()
+        split_y(far, 1)
 
     @pl.when(inside)
     def _():
@@ -391,8 +407,7 @@
         rs_take(side_in, z)
         rs_take(side_out, z)
         send_stats(0)
-        full_y(outer, 1)
-        t_swap(1).start()
+        split_y(outer, 1)
 
     def lp():
         return rc(lossb.at[0], lossb.at[1], ls_s.at[nt], ls_r.at[nt], partner)

time: 76.8 us -> 76.3 us (level)
  no operation moved by 1% of the time
where the time goes in v4:
time: 76.3 us; the launch traced here: 76.1 us
  Pallas kernels  74.3 us (97%)
  between operations  1.16 us (2%)
    pallas_call x1, Pallas kernels, fused_shards(): pl.pallas_call(functools.partial(fused, n, nt, ng), out_shape=(pltpu.VMEM...  74.3 us

profile of v4, /device:TPU:1, one launch (start us, length us, event | category | flops | bytes accessed | tf_op | source)
XLA Modules:
  0.0 76.1 jit_solution(10779965724639025054)
XLA Ops:
  0.6 74.3 %divergence_grad.1 = (bf16[128,1024]{1,0:T(8,128)(2,1)S(1)}, f32[1,1]{1,0:T(1,128)S(4)}) custom-call(bf16[128,1024]{1,0:T(8,128)(2,1)} %x_hbm.1, bf16[128,2048]{1,0:T(8,128)(2,1)} %y_hbm.1, f32[1,128]{1,0:T(1,128)} %bitcast.2, bf16[4096,512]{1,0:T(8,128)(2,1)} %sw_hbm.1, bf16[8192,512]{1,0:T(8,128)(2,1)} %tw_hbm.1), custom_call_target="tpu_custom_call" | custom-call | tf_op jit(solution)/shard_map/divergence_grad/pallas_call | solution.py:470
  75.4 0.7 copy.9

commit v5 on v4

--- a/solution.py
+++ b/solution.py
@@ -172,16 +172,10 @@
         teacher_dot(tg.at[i], i, g, False)
 
     def split_y(i, g):
-        step = kt // 2
         for c in range(2):
             take_y(i, g, c)
             mine_gc = pl.ds(pl.multiple_of(owner[c] * q, q), q)
-
-            @pl.loop(0, 2)
-            def _(s):
-                cols = pl.ds(pl.multiple_of(s * step, step), step)
-                term = jnp.dot(tg[i, group(owner[c], g), cols], tw[i, cols, :], preferred_element_type=F32)
-                tacc[g, mine_gc, :] += term
+            tacc[g, mine_gc, :] += jnp.dot(tg[i, group(owner[c], g), :], tw[i], preferred_element_type=F32)
             if c == 0:
                 t_swap(g).start()
 
@@ -191,8 +185,9 @@
         dot_y(i, g)
 
     def student(j):
-        sp[j] = jnp.dot(x_ref[...], wf[j], preferred_element_type=F32)
+        sp[j, theirs, :] = jnp.dot(x_ref[theirs, :], wf[j], preferred_element_type=F32)
         rc(sp.at[j, theirs], spx.at[j], px_s.at[j], px_r.at[j], partner).start()
+        sp[j, mine, :] = jnp.dot(x_ref[mine, :], wf[j], preferred_element_type=F32)
 
     def student_sum(j):
         rc(sp.at[j, theirs], spx.at[j], px_s.at[j], px_r.at[j], partner).wait_recv()

time: 76.3 us -> 76.2 us (level)
  no operation moved by 1% of the time
where the time goes in v5:
time: 76.2 us; the launch traced here: 76 us
  Pallas kernels  74.1 us (97%)
  between operations  1.16 us (2%)
    pallas_call x1, Pallas kernels, fused_shards(): pl.pallas_call(functools.partial(fused, n, nt, ng), out_shape=(pltpu.VMEM...  74.1 us

profile of v5, /device:TPU:1, one launch (start us, length us, event | category | flops | bytes accessed | tf_op | source)
XLA Modules:
  0.0 76.0 jit_solution(16508556479454476639)
XLA Ops:
  0.6 74.1 %divergence_grad.1 = (bf16[128,1024]{1,0:T(8,128)(2,1)S(1)}, f32[1,1]{1,0:T(1,128)S(4)}) custom-call(bf16[128,1024]{1,0:T(8,128)(2,1)} %x_hbm.1, bf16[128,2048]{1,0:T(8,128)(2,1)} %y_hbm.1, f32[1,128]{1,0:T(1,128)} %bitcast.2, bf16[4096,512]{1,0:T(8,128)(2,1)} %sw_hbm.1, bf16[8192,512]{1,0:T(8,128)(2,1)} %tw_hbm.1), custom_call_target="tpu_custom_call" | custom-call | tf_op jit(solution)/shard_map/divergence_grad/pallas_call | solution.py:465
  75.3 0.7 copy.9
